TPU v7x, 256 devices: a whole 4x4x8 slice. The times are simulated.
256 devices in a mesh: dp: 64 (over y, z, core), member: 4 (over x).
Axes of the slice: x: 4, y: 4, z: 8, core: 2. Of those that a mesh axis runs over, the one named last changes fastest.
Arguments:
- features: bfloat16 [32768, 256], P('dp'), may hold values from -6 to 6
- next_features: bfloat16 [32768, 256], P('dp'), may hold values from -6 to 6
- rewards: bfloat16 [32768], P('dp'), may hold values from -6 to 6
- next_logp: bfloat16 [32768], P('dp'), may hold values from -8 to 8
- terminal: int32 [32768], P('dp'), may hold values 0 or 1
- source_ids: int32 [32768], P('dp'), may hold values from 0 to 7
- source_weight: bfloat16 [8], replicated, may hold values from 0.29882812 to 3
- subset: int32 [32768, 2], P('dp'), may hold values from 0 to 7, all different within a row
- destination: int32 [32768], P('dp'), may hold values from 0 to 63, as said below
- critic_w1: float32 [8, 2048, 256], P('member'), may hold values from -0.375 to 0.375
- critic_shift: float32 [8, 2048], P('member'), may hold values from -3 to 3
- critic_head: float32 [8, 2048], P('member'), may hold values from -0.125 to 0.125
- target_w1: bfloat16 [8, 2048, 256], P('member'), may hold values from -0.375 to 0.375
- target_mean: float32 [8, 2048], P('member'), may hold values from -2 to 2
- target_scale: float32 [8, 2048], P('member'), may hold values from 0.5 to 2
- target_shift: float32 [8, 2048], P('member'), may hold values from -3 to 3
- target_head: float32 [8, 2048], P('member'), may hold values from -0.125 to 0.125
Outputs:
- step_w1: float32 [8, 2048, 256], P('member')
- step_shift: float32 [8, 2048], P('member')
- step_head: float32 [8, 2048], P('member')
Inputs may be any that keep to these rules, and one draw needn't show every extreme that they name: `destination`: in the 512 transitions that start on one index of dp, every shard is named at least 512 // 128 times and at most 16 times, and some shard exactly 16 times. `subset`: the entries of a row differ.
All inputs are finite; a program needn't handle non-finite values. No bound on the sum of `terminal` on one device may be relied on, other than what follows from the above.
Results may differ from a plain program's by a relative error of at most 0.003.
The roundings to bfloat16 on the way count: a program that leaves them out, or rounds other values in their place, can miss the bound.
Values may be sent and summed in bfloat16 or wider, within the bound.
A program may use at most 128 MiB of HBM per device.

v0:
```python
import math
import jax
import jax.numpy as jnp
from jax import lax
from jax.sharding import PartitionSpec as P

GAMMA = 0.99
ALPHA = 0.2
EPS = 1e-05


def in_one(arrays, axis):
    ends = [0]
    for a in arrays:
        ends.append(ends[-1] + a.size)
    running = lax.psum(jnp.concatenate([a.ravel() for a in arrays]), axis)
    return tuple((running[b:e].reshape(a.shape) for a, b, e in zip(arrays, ends, ends[1:])))


def sent_to_all(array, axis):
    copies = jnp.broadcast_to(array, (lax.axis_size(axis), *array.shape))
    return lax.all_to_all(copies, axis, split_axis=0, concat_axis=0, tiled=True)


def over_copies(array, axis):
    everything = sent_to_all(array, axis)
    return jnp.sum(everything, axis=0)


def per_device(
    features,
    next_features,
    rewards,
    next_logp,
    terminal,
    source_ids,
    source_weight,
    subset,
    destination,
    critic_w1,
    critic_shift,
    critic_head,
    target_w1,
    target_mean,
    target_scale,
    target_shift,
    target_head,
):
    shards = lax.axis_size("dp")
    members = lax.axis_size("member")
    local_rows = features.shape[0]
    width = features.shape[1]
    local_critics = critic_w1.shape[0]
    total_critics = local_critics * members
    capacity = 2 * local_rows // shards
    slot_total = shards * capacity
    shard_iota = jnp.arange(shards, dtype=jnp.int32)
    picked = (destination[:, None] == shard_iota[None]).astype(jnp.int32)
    earlier = jnp.cumsum(picked, axis=0) - picked
    rank = jnp.sum(earlier * picked, axis=1)
    position = destination * capacity + rank

    def place(values):
        empty = jnp.zeros((slot_total,) + values.shape[1:], values.dtype)
        return empty.at[position].set(values).reshape((shards, capacity) + values.shape[1:])

    source_iota = jnp.arange(source_weight.shape[0], dtype=jnp.int32)
    weight_rows = jnp.sum(
        jnp.where(
            source_ids[:, None] == source_iota[None], source_weight.astype(jnp.float32)[None], 0.0
        ),
        axis=1,
    ).astype(jnp.bfloat16)
    carry_rows = (1 - terminal).astype(jnp.bfloat16)
    pre_act = jnp.einsum(
        "si,cfi->csf", next_features, target_w1, preferred_element_type=jnp.float32
    )
    active = jnp.maximum(
        (pre_act - target_mean[:, None]) * target_scale[:, None] + target_shift[:, None], 0.0
    )
    mine = jnp.sum(active * target_head[:, None], axis=2).T
    everyone = lax.all_gather(mine, "member", axis=1, tiled=True)
    critic_iota = jnp.arange(total_critics, dtype=jnp.int32)
    first = jnp.sum(jnp.where(subset[:, 0][:, None] == critic_iota[None], everyone, 0.0), axis=1)
    second = jnp.sum(jnp.where(subset[:, 1][:, None] == critic_iota[None], everyone, 0.0), axis=1)
    lowest = jnp.minimum(first, second)
    value = rewards.astype(jnp.float32) + GAMMA * carry_rows.astype(jnp.float32) * (
        lowest - ALPHA * next_logp.astype(jnp.float32)
    )
    value = value.astype(jnp.bfloat16)
    received, weight_slots, target_slots = (
        lax.all_to_all(place(features), "dp", split_axis=0, concat_axis=0, tiled=True),
        lax.all_to_all(place(weight_rows), "dp", split_axis=0, concat_axis=0, tiled=True),
        lax.all_to_all(place(value), "dp", split_axis=0, concat_axis=0, tiled=True),
    )
    rows_in = received.reshape(slot_total, width)
    weight = weight_slots.reshape(slot_total).astype(jnp.float32)
    target = target_slots.reshape(slot_total).astype(jnp.float32)
    live = (weight > 0).astype(jnp.float32)
    live_count = jnp.sum(live)
    live_col = live[:, None]

    def critic(params):
        weights, offset, output = params
        pre_act = jnp.dot(
            rows_in, weights.astype(jnp.bfloat16).T, preferred_element_type=jnp.float32
        )
        centred = pre_act - jnp.sum(pre_act * live_col, axis=0, keepdims=True) / live_count
        inverse = 1.0 / jnp.sqrt(
            jnp.sum(centred * centred * live_col, axis=0, keepdims=True) / live_count + EPS
        )
        normed = centred * inverse
        before = normed + offset[None]
        active = jnp.maximum(before, 0.0)
        value_now = jnp.sum(active * output[None], axis=1)
        slope = weight * (value_now - target)
        grad_head = jnp.dot(slope, active)
        grad_unit = jnp.where(before > 0, slope[:, None] * output[None], 0.0)
        grad_shift = jnp.sum(grad_unit, axis=0)
        unit_mean = jnp.sum(grad_unit * live_col, axis=0, keepdims=True) / live_count
        cross_mean = jnp.sum(grad_unit * normed * live_col, axis=0, keepdims=True) / live_count
        grad_pre = (inverse * (grad_unit - unit_mean - normed * cross_mean) * live_col).astype(
            jnp.bfloat16
        )
        grad_w1 = jnp.dot(grad_pre.T, rows_in, preferred_element_type=jnp.float32)
        return (grad_w1, grad_shift, grad_head)

    grad_w1, grad_shift, grad_head = lax.map(critic, (critic_w1, critic_shift, critic_head))
    hidden = critic_w1.shape[1]
    root = jnp.float32(math.sqrt(total_critics * hidden * (width + 2)))
    grad_w1, grad_shift, grad_head = in_one((grad_w1, grad_shift, grad_head), "dp")
    squares = (
        jnp.sum(grad_w1 * grad_w1)
        + jnp.sum(grad_shift * grad_shift)
        + jnp.sum(grad_head * grad_head)
    )
    norm = jnp.sqrt(over_copies(squares, "member"))
    factor = root / jnp.maximum(norm, root)
    return (grad_w1 * factor, grad_shift * factor, grad_head * factor)


def solution(mesh):
    in_specs = (
        P("dp", None),
        P("dp", None),
        P("dp"),
        P("dp"),
        P("dp"),
        P("dp"),
        P(),
        P("dp", None),
        P("dp"),
        P("member", None, None),
        P("member", None),
        P("member", None),
        P("member", None, None),
        P("member", None),
        P("member", None),
        P("member", None),
        P("member", None),
    )
    out_specs = (P("member", None, None), P("member", None), P("member", None))
    return jax.shard_map(
        per_device, mesh=mesh, in_specs=in_specs, out_specs=out_specs, check_vma=False
    )
```

profile of v0, /device:TPU:8, one launch (start us, length us, event | category | flops | bytes accessed | tf_op | source)
XLA Modules:
  0.0 378.9 jit_solution(3712643342671129567)
XLA Ops:
  8.8 4.7 %multiply_reduce_fusion.4 = f32[2,512]{1,0:T(2,128)S(1)} fusion(bf16[2,2048,256]{2,1,0:T(8,128)(2,1)S(1)} %copy-done, f32[2,2048]{1,0:T(2,128)} %param.35, f32[2,2048]{1,0:T(2,128)} %param.34, f32[2,2048]{1,0:T(2,128)} %param.33, f32[2,2048]{1,0:T(2,128)} %param.32, bf16[512,256]{1,0:T(8,128)(2,1)} %param.20), kind=kOutput, calls=%fused_computation.42 | convolution fusion | flops 1086323712 | bytes 2428928 | tf_op jit(solution)/shard_map/si,cfi->csf/dot_general | solution.py:75
  13.6 12.4 %all-gather = f32[4,2,512]{2,1,0:T(2,128)S(1)} all-gather(f32[1,2,512]{2,1,0:T(2,128)S(1)} %bitcast.140), channel_id=1, replica_groups=mesh['dp'=64,'member'=4] {'member'}, dimensions={0}, use_global_device_ids=true | all-gather | bytes 20480 | tf_op jit(solution)/shard_map/all_gather | solution.py:82
  26.0 1.2 reduce-window.6
  27.7 3.8 scatter_custom_fusion.2
  32.2 12.1 %all-to-all-start.2 = ((bf16[64,1,16]{2,1,0:T(2,128)(2,1)}), bf16[64,1,16]{2,1,0:T(2,128)(2,1)S(1)}, u32[]{:S(2)}, u32[]{:S(2)}) async-start(bf16[64,1,16]{2,1,0:T(2,128)(2,1)} %all_to_all.26), calls=%async_computation.2 | async-start | bytes 65536 | tf_op jit(solution)/shard_map/all_to_all | solution.py:94
  44.4 3.8 scatter_custom_fusion.1
  48.9 4.0 %all-to-all-done.2 = bf16[64,1,16]{2,1,0:T(2,128)(2,1)S(1)} async-done(((bf16[64,1,16]{2,1,0:T(2,128)(2,1)}), bf16[64,1,16]{2,1,0:T(2,128)(2,1)S(1)}, u32[]{:S(2)}, u32[]{:S(2)}) %all-to-all-start.2) | async-done | bytes 2080 | tf_op jit(solution)/shard_map/all_to_all | solution.py:94
  52.9 6.3 %all-to-all-start.1 = ((bf16[64,1,16]{2,1,0:T(2,128)(2,1)}), bf16[64,1,16]{2,1,0:T(2,128)(2,1)S(1)}, u32[]{:S(2)}, u32[]{:S(2)}) async-start(bf16[64,1,16]{2,1,0:T(2,128)(2,1)} %all_to_all.25), calls=%async_computation.1 | async-start | bytes 65536 | tf_op jit(solution)/shard_map/all_to_all | solution.py:93
  59.2 3.5 scatter_custom_fusion
  62.7 5.0 %all-to-all-done.1 = bf16[64,1,16]{2,1,0:T(2,128)(2,1)S(1)} async-done(((bf16[64,1,16]{2,1,0:T(2,128)(2,1)}), bf16[64,1,16]{2,1,0:T(2,128)(2,1)S(1)}, u32[]{:S(2)}, u32[]{:S(2)}) %all-to-all-start.1) | async-done | bytes 2080 | tf_op jit(solution)/shard_map/all_to_all | solution.py:93
  67.8 5.5 %all-to-all-start = ((bf16[64,16,256]{2,1,0:T(8,128)(2,1)}), bf16[64,16,256]{2,1,0:T(8,128)(2,1)S(1)}, u32[]{:S(2)}, u32[]{:S(2)}) async-start(bf16[64,16,256]{2,1,0:T(8,128)(2,1)} %bitcast.11), calls=%async_computation | async-start | bytes 1048576 | tf_op jit(solution)/shard_map/all_to_all | solution.py:92
  73.4 3.8 convert.6
  78.3 11.7 %all-to-all-done = bf16[64,16,256]{2,1,0:T(8,128)(2,1)S(1)} async-done(((bf16[64,16,256]{2,1,0:T(8,128)(2,1)}), bf16[64,16,256]{2,1,0:T(8,128)(2,1)S(1)}, u32[]{:S(2)}, u32[]{:S(2)}) %all-to-all-start) | async-done | bytes 524320 | tf_op jit(solution)/shard_map/all_to_all | solution.py:92
  90.0 50.4 %while.14 = (s32[]{:T(128)}, f32[2,2048,256]{2,1,0:T(8,128)}, f32[2,2048]{1,0:T(2,128)S(1)}, f32[2,2048]{1,0:T(2,128)S(1)}, bf16[2,2048,256]{2,1,0:T(8,128)(2,1)...) while((s32[]{:T(128)}, f32[2,2048,256]{2,1,0:T(8,128)}, ...), condition=%wide.region_18.19_spmd, body=%wide.region_11.18_spmd.sunk | while | flops 2231370752 | bytes 92651704 | solution.py:128
  90.0 2.5 multiply_reduce_fusion.12
  95.1 2.1 multiply_reduce_fusion.14
  97.2 1.4 fusion.63
  98.6 7.7 %multiply_reduce_fusion.15 = (f32[2048]{0:T(1024)S(1)}, f32[2048]{0:T(1024)S(1)}, f32[2048]{0:T(1024)S(1)}, pred[1024,2048]{1,0:T(32,128)(4,1)}) fusion(f32[1024]{0:T(1024)S(1)} %bitcast.129, f32[1024]{0:T(1024)S(1)} %subtract_multiply_fusion.4, f32[2048]{0:T(1024)S(1)} %bitcast.125, f32[2048]{0:T(1024)S(1)} %add_rsqrt_fusion.2, ...), kind=kLoop, calls=%fused_computation.12.clone.1 | loop fusion | flops 25159680 | bytes 10551296 | tf_op jit(solution)/shard_map/while/body/eval_jaxpr/reduce_sum | solution.py:120
  107.0 8.2 %fusion.62 = f32[2,2048,256]{2,1,0:T(8,128)} fusion(f32[2,2048,256]{2,1,0:T(8,128)} %get-tuple-element.217, s32[]{:T(128)S(6)} %copy.44, bf16[1024,256]{1,0:T(8,128)(2,1)S(1)} %get-tuple-element.235, pred[1024,2048]{1,0:T(32,128)(4,1)} %get-tuple-element.196, f32[2048,1024]{0,1:T(8,128)} %copy-done.1, f32[2048]{0:T(1024)S(1)} %get-tuple-element.199, ...), kind=kOutput, calls=%fused_computation.28.clone.1 | convolution fusion | flops 1094713344 | bytes 13164548 | tf_op jit(solution)/shard_map/while/body/eval_jaxpr/dot_general | solution.py:125
  115.2 2.5 multiply_reduce_fusion.12
  120.3 2.1 multiply_reduce_fusion.14
  122.4 1.4 fusion.63
  123.8 7.7 %multiply_reduce_fusion.15 = (f32[2048]{0:T(1024)S(1)}, f32[2048]{0:T(1024)S(1)}, f32[2048]{0:T(1024)S(1)}, pred[1024,2048]{1,0:T(32,128)(4,1)}) fusion(f32[1024]{0:T(1024)S(1)} %bitcast.129, f32[1024]{0:T(1024)S(1)} %subtract_multiply_fusion.4, f32[2048]{0:T(1024)S(1)} %bitcast.125, f32[2048]{0:T(1024)S(1)} %add_rsqrt_fusion.2, ...), kind=kLoop, calls=%fused_computation.12.clone.1 | loop fusion | flops 25159680 | bytes 10551296 | tf_op jit(solution)/shard_map/while/body/eval_jaxpr/reduce_sum | solution.py:120
  132.2 8.2 %fusion.62 = f32[2,2048,256]{2,1,0:T(8,128)} fusion(f32[2,2048,256]{2,1,0:T(8,128)} %get-tuple-element.217, s32[]{:T(128)S(6)} %copy.44, bf16[1024,256]{1,0:T(8,128)(2,1)S(1)} %get-tuple-element.235, pred[1024,2048]{1,0:T(32,128)(4,1)} %get-tuple-element.196, f32[2048,1024]{0,1:T(8,128)} %copy-done.1, f32[2048]{0:T(1024)S(1)} %get-tuple-element.199, ...), kind=kOutput, calls=%fused_computation.28.clone.1 | convolution fusion | flops 1094713344 | bytes 13164548 | tf_op jit(solution)/shard_map/while/body/eval_jaxpr/dot_general | solution.py:125
  140.4 4.3 %copy.33 = f32[512,2,8,128]{3,1,2,0:T(2,128)S(1)} copy(f32[512,2,8,128]{3,2,1,0:T(8,128)} %bitcast.120) | data formatting | bytes 8388608
  144.8 4.4 %pad_maximum_fusion = f32[1056768]{0:T(1024)} fusion(f32[4096]{0:T(1024)S(1)} %bitcast.133, f32[4096]{0:T(1024)S(1)} %bitcast.134, f32[1048576]{0:T(1024)S(1)} %bitcast.119), kind=kLoop, calls=%fused_computation.43 | loop fusion | flops 2113536 | bytes 8454144 | tf_op jit(solution)/shard_map/concatenate | solution.py:16
  149.2 193.5 %all-reduce.2.cloned.1.call-done = f32[1056768]{0:T(1024)} async-done(((f32[1056768]{0:T(1024)}), f32[1056768]{0:T(1024)}) %all-reduce.2.cloned.1.call-update) | async-done | bytes 4227088 | tf_op jit(solution)/shard_map/psum | solution.py:16
  342.6 3.9 %multiply_reduce_fusion.5 = f32[]{:T(128)} fusion(f32[1056768]{0:T(1024)} %all-reduce.2.cloned.1.call-done), kind=kLoop, calls=%fused_computation.44 | loop fusion | flops 2097151 | bytes 4194308 | tf_op jit(solution)/shard_map/reduce_sum | solution.py:133
  346.5 1.3 multiply_reduce_fusion.6
  349.8 9.3 %all_to_all.31 = f32[4,1,1]{2,1,0:T(1,128)S(1)} all-to-all(f32[4,1,1]{2,1,0:T(1,128)S(1)} %broadcast_in_dim.49), channel_id=1, replica_groups=mesh['dp'=64,'member'=4] {'member'}, dimensions={0} | all-to-all | bytes 32 | tf_op jit(solution)/shard_map/all_to_all | solution.py:22
  360.5 4.4 %slice_multiply_fusion = f32[1048576]{0:T(1024)} fusion(f32[1056768]{0:T(1024)} %all-reduce.2.cloned.1.call-done, f32[]{:T(128)S(6)} %div.42), kind=kLoop, calls=%fused_computation.45 | loop fusion | flops 1048576 | bytes 8388612 | tf_op jit(solution)/shard_map/mul | solution.py:139
  364.9 5.2 %mul.195 = f32[2,2048,256]{2,1,0:T(8,128)} reshape(f32[1048576]{0:T(1024)} %slice_multiply_fusion) | data formatting | bytes 8388608 | tf_op jit(solution)/shard_map/mul | solution.py:139
  (71 shorter events, 14.0 us)
Async XLA Ops:
  7.2 1.6 copy-start
  8.8 17.2 %copy-start.4 = (s32[512]{0:T(512)S(1)}, s32[512]{0:T(512)}, u32[]{:S(2)}) copy-start(s32[512]{0:T(512)} %param.27) | copy-start | bytes 6148
  8.8 18.9 %copy-start.6 = (s32[512]{0:T(512)S(1)}, s32[512]{0:T(512)}, u32[]{:S(2)}) copy-start(s32[512]{0:T(512)} %param.23) | copy-start | bytes 6148
  8.8 18.9 %copy-start.7 = (bf16[512]{0:T(512)(128)(2,1)S(1)}, bf16[512]{0:T(512)(128)(2,1)}, u32[]{:S(2)}) copy-start(bf16[512]{0:T(512)(128)(2,1)} %param.22) | copy-start | bytes 3076
  8.8 18.9 %copy-start.8 = (bf16[512]{0:T(512)(128)(2,1)S(1)}, bf16[512]{0:T(512)(128)(2,1)}, u32[]{:S(2)}) copy-start(bf16[512]{0:T(512)(128)(2,1)} %param.21) | copy-start | bytes 3076
  8.8 35.5 %copy-start.9 = (bf16[8]{0:T(256)(128)(2,1)S(1)}, bf16[8]{0:T(256)(128)(2,1)}, u32[]{:S(2)}) copy-start(bf16[8]{0:T(256)(128)(2,1)} %param.25) | copy-start | bytes 52
  8.8 35.5 %copy-start.5 = (s32[512]{0:T(512)S(1)}, s32[512]{0:T(512)}, u32[]{:S(2)}) copy-start(s32[512]{0:T(512)} %param.24) | copy-start | bytes 6148
  13.6 76.4 %copy-start.2 = (f32[2,2048]{1,0:T(2,128)S(1)}, f32[2,2048]{1,0:T(2,128)}, u32[]{:S(2)}) copy-start(f32[2,2048]{1,0:T(2,128)} %param.29) | copy-start | bytes 49156
  13.6 76.4 %copy-start.3 = (f32[2,2048]{1,0:T(2,128)S(1)}, f32[2,2048]{1,0:T(2,128)}, u32[]{:S(2)}) copy-start(f32[2,2048]{1,0:T(2,128)} %param.30) | copy-start | bytes 49156
  32.2 20.7 %all-to-all-start.2 = ((bf16[64,1,16]{2,1,0:T(2,128)(2,1)}), bf16[64,1,16]{2,1,0:T(2,128)(2,1)S(1)}, u32[]{:S(2)}, u32[]{:S(2)}) async-start(bf16[64,1,16]{2,1,0:T(2,128)(2,1)} %all_to_all.26), calls=%async_computation.2 | async-start | bytes 65536 | tf_op jit(solution)/shard_map/all_to_all | solution.py:94
  52.9 14.9 %all-to-all-start.1 = ((bf16[64,1,16]{2,1,0:T(2,128)(2,1)}), bf16[64,1,16]{2,1,0:T(2,128)(2,1)S(1)}, u32[]{:S(2)}, u32[]{:S(2)}) async-start(bf16[64,1,16]{2,1,0:T(2,128)(2,1)} %all_to_all.25), calls=%async_computation.1 | async-start | bytes 65536 | tf_op jit(solution)/shard_map/all_to_all | solution.py:93
  67.8 22.2 %all-to-all-start = ((bf16[64,16,256]{2,1,0:T(8,128)(2,1)}), bf16[64,16,256]{2,1,0:T(8,128)(2,1)S(1)}, u32[]{:S(2)}, u32[]{:S(2)}) async-start(bf16[64,16,256]{2,1,0:T(8,128)(2,1)} %bitcast.11), calls=%async_computation | async-start | bytes 1048576 | tf_op jit(solution)/shard_map/all_to_all | solution.py:92
  73.3 269.3 %all-reduce.2.cloned.1.call-start = ((), (), s32[]{:S(2)}) async-start(), calls=%async_computation.4 | async-start | bytes 8454144 | tf_op jit(solution)/shard_map/psum | solution.py:16
  92.6 4.6 %copy-start.1 = (f32[2048,1024]{0,1:T(8,128)}, f32[2048,1024]{0,1:T(8,128)S(1)}, u32[]{:S(2)}) copy-start(f32[2048,1024]{0,1:T(8,128)S(1)} %get-tuple-element.194) | copy-start | bytes 25165828 | tf_op jit(solution)/shard_map/while
  117.8 4.6 %copy-start.1 = (f32[2048,1024]{0,1:T(8,128)}, f32[2048,1024]{0,1:T(8,128)S(1)}, u32[]{:S(2)}) copy-start(f32[2048,1024]{0,1:T(8,128)S(1)} %get-tuple-element.194) | copy-start | bytes 25165828 | tf_op jit(solution)/shard_map/while
Sparse Core Ops, SparseCore 0:
  149.3 193.2 all-reduce.1
where the time goes:
time: 380 us; the launch traced here: 379 us
  waiting for transfers between devices  214 us (56%)
  other arithmetic  47.4 us (12%)
  matrix products  28.9 us (8%)
  local copies, waits for them, and re-layouts  25.7 us (7%)
  starting transfers between devices  24 us (6%)
  blocking collectives  21.7 us (6%)
  between operations  16.9 us (4%)
    psum x1, waiting for transfers between devices, in_one(): running = lax.psum(jnp.concatenate([a.ravel() for a in arrays]), axis)  193 us
    dot_general x2, matrix products, critic(): grad_w1 = jnp.dot(grad_pre.T, rows_in, preferred_element_type=jnp.float32)  16.4 us
    reduce_sum x2, other arithmetic, critic(): jnp.sum(grad_unit * live_col, axis=0, keepdims=True) / live_count  15.4 us
    all_gather x1, blocking collectives, per_device(): everyone = lax.all_gather(mine, 'member', axis=1, tiled=True)  12.4 us
    all_to_all x1, starting transfers between devices, per_device(): lax.all_to_all(place(value), 'dp', split_axis=0, concat_axis=0, tiled=True)  12.1 us
    all_to_all x1, waiting for transfers between devices, per_device(): lax.all_to_all(place(features), 'dp', split_axis=0, concat_axis=0, tiled=...  11.7 us
    scatter x3, local copies, waits for them, and re-layouts, place(): empty.at[position].set(values)  11.1 us
    all_to_all x1, blocking collectives, sent_to_all(): return lax.all_to_all(copies, axis, split_axis=0, concat_axis=0, tiled=True)  9.33 us
  transfers between devices with their start and end apart: 4, of which 4 were waited for; matrix products, arithmetic and copies ran while one was open for 3% of the time, Pallas kernels for 0%

commit v1 on v0

--- a/solution.py
+++ b/solution.py
@@ -79,7 +79,9 @@
         (pre_act - target_mean[:, None]) * target_scale[:, None] + target_shift[:, None], 0.0
     )
     mine = jnp.sum(active * target_head[:, None], axis=2).T
-    everyone = lax.all_gather(mine, "member", axis=1, tiled=True)
+    everyone = jnp.concatenate(
+        lax.all_to_all(jnp.stack([mine] * lax.axis_size("member")), "member", 0, 0), axis=1
+    )
     critic_iota = jnp.arange(total_critics, dtype=jnp.int32)
     first = jnp.sum(jnp.where(subset[:, 0][:, None] == critic_iota[None], everyone, 0.0), axis=1)
     second = jnp.sum(jnp.where(subset[:, 1][:, None] == critic_iota[None], everyone, 0.0), axis=1)

time: 380 us -> 374 us (0.984)
  blocking collectives: 21.7 us -> 9.33 us
  starting transfers between devices: 24 us -> 28.4 us
    all_gather x1 -> x0, blocking collectives: 12.4 us -> none  [per_device(): everyone = lax.all_gather(mine, 'member', axis=1, tiled=True)]
    all_to_all x1, starting transfers between devices: 6.34 us -> 12.1 us  [per_device(): lax.all_to_all(place(weight_rows), 'dp', split_axis=0, concat_axis=0, til...]
    all_to_all x1, starting transfers between devices: 12.1 us -> 6.4 us  [per_device(): lax.all_to_all(place(value), 'dp', split_axis=0, concat_axis=0, tiled=True)]
    all_to_all x0 -> x1, starting transfers between devices: none -> 4.3 us  [per_device(): lax.all_to_all(jnp.stack([mine] * lax.axis_size('member')), 'member', 0, 0)]
  transfers between devices with their start and end apart: 4 -> 5, of which waited for: 4 -> 4; matrix products, arithmetic and copies ran while one was open for 3% -> 5% of each run, Pallas kernels for 0% -> 0%
where the time goes in v1:
time: 374 us; the launch traced here: 373 us
  waiting for transfers between devices  215 us (57%)
  other arithmetic  47.4 us (13%)
  matrix products  28.8 us (8%)
  starting transfers between devices  28.4 us (8%)
  local copies, waits for them, and re-layouts  26.2 us (7%)
  between operations  17 us (5%)
  blocking collectives  9.33 us (2%)
    psum x1, waiting for transfers between devices, in_one(): running = lax.psum(jnp.concatenate([a.ravel() for a in arrays]), axis)  195 us
    dot_general x2, matrix products, critic(): grad_w1 = jnp.dot(grad_pre.T, rows_in, preferred_element_type=jnp.float32)  16.4 us
    reduce_sum x2, other arithmetic, critic(): jnp.sum(grad_unit * live_col, axis=0, keepdims=True) / live_count  15.4 us
    all_to_all x1, starting transfers between devices, per_device(): lax.all_to_all(place(weight_rows), 'dp', split_axis=0, concat_axis=0, til...  12.1 us
    all_to_all x1, waiting for transfers between devices, per_device(): lax.all_to_all(place(features), 'dp', split_axis=0, concat_axis=0, tiled=...  11.7 us
    scatter x3, local copies, waits for them, and re-layouts, place(): empty.at[position].set(values)  11.1 us
    all_to_all x1, blocking collectives, sent_to_all(): return lax.all_to_all(copies, axis, split_axis=0, concat_axis=0, tiled=True)  9.33 us
  transfers between devices with their start and end apart: 5, of which 4 were waited for; matrix products, arithmetic and copies ran while one was open for 5% of the time, Pallas kernels for 0%

profile of v1, /device:TPU:8, one launch (start us, length us, event | category | flops | bytes accessed | tf_op | source)
XLA Modules:
  0.0 372.6 jit_solution(14756329088967809607)
XLA Ops:
  7.3 1.5 copy-done
  8.8 4.7 %multiply_reduce_fusion.4 = f32[2,512]{1,0:T(2,128)S(1)} fusion(bf16[2,2048,256]{2,1,0:T(8,128)(2,1)S(1)} %copy-done, f32[2,2048]{1,0:T(2,128)} %param.35, f32[2,2048]{1,0:T(2,128)} %param.34, f32[2,2048]{1,0:T(2,128)} %param.33, f32[2,2048]{1,0:T(2,128)} %param.32, bf16[512,256]{1,0:T(8,128)(2,1)} %param.20), kind=kOutput, calls=%fused_computation.42 | convolution fusion | flops 1086323712 | bytes 2428928 | tf_op jit(solution)/shard_map/si,cfi->csf/dot_general | solution.py:75
  14.1 4.3 %all-to-all-start.2 = ((f32[4,512,2]{1,2,0:T(2,128)}), f32[4,512,2]{1,2,0:T(2,128)S(1)}, u32[]{:S(2)}, u32[]{:S(2)}) async-start(f32[4,512,2]{1,2,0:T(2,128)} %stack.2), calls=%async_computation.2 | async-start | bytes 32768 | tf_op jit(solution)/shard_map/all_to_all | solution.py:83
  20.2 3.8 %scatter_custom_fusion.1 = bf16[1024]{0:T(1024)(128)(2,1)S(1)} fusion(s32[512]{0:T(512)S(1)} %compare_select_fusion.2, bf16[512]{0:T(512)(128)(2,1)S(1)} %select_reduce_fusion, bf16[]{:T(256)} %constant.22.clone.1), kind=kCustom, calls=%fused_computation.79 | custom fusion | bytes 2050 | tf_op jit(solution)/shard_map/scatter | solution.py:65
  24.6 12.1 %all-to-all-start.1 = ((bf16[64,1,16]{2,1,0:T(2,128)(2,1)}), bf16[64,1,16]{2,1,0:T(2,128)(2,1)S(1)}, u32[]{:S(2)}, u32[]{:S(2)}) async-start(bf16[64,1,16]{2,1,0:T(2,128)(2,1)} %all_to_all.29), calls=%async_computation.1 | async-start | bytes 65536 | tf_op jit(solution)/shard_map/all_to_all | solution.py:95
  36.9 3.8 %scatter_custom_fusion.2 = bf16[1024]{0:T(1024)(128)(2,1)S(1)} fusion(s32[512]{0:T(512)S(1)} %compare_select_fusion.2, bf16[512]{0:T(512)(128)(2,1)S(1)} %add_convert_fusion, bf16[]{:T(256)} %constant.22.clone.1), kind=kCustom, calls=%fused_computation.77 | custom fusion | bytes 2050 | tf_op jit(solution)/shard_map/scatter | solution.py:65
  41.4 3.9 %all-to-all-done.1 = bf16[64,1,16]{2,1,0:T(2,128)(2,1)S(1)} async-done(((bf16[64,1,16]{2,1,0:T(2,128)(2,1)}), bf16[64,1,16]{2,1,0:T(2,128)(2,1)S(1)}, u32[]{:S(2)}, u32[]{:S(2)}) %all-to-all-start.1) | async-done | bytes 2080 | tf_op jit(solution)/shard_map/all_to_all | solution.py:95
  45.3 6.4 %all-to-all-start.3 = ((bf16[64,1,16]{2,1,0:T(2,128)(2,1)}), bf16[64,1,16]{2,1,0:T(2,128)(2,1)S(1)}, u32[]{:S(2)}, u32[]{:S(2)}) async-start(bf16[64,1,16]{2,1,0:T(2,128)(2,1)} %all_to_all.30), calls=%async_computation.3 | async-start | bytes 65536 | tf_op jit(solution)/shard_map/all_to_all | solution.py:96
  51.7 3.5 scatter_custom_fusion
  55.2 5.1 %all-to-all-done.3 = bf16[64,1,16]{2,1,0:T(2,128)(2,1)S(1)} async-done(((bf16[64,1,16]{2,1,0:T(2,128)(2,1)}), bf16[64,1,16]{2,1,0:T(2,128)(2,1)S(1)}, u32[]{:S(2)}, u32[]{:S(2)}) %all-to-all-start.3) | async-done | bytes 2080 | tf_op jit(solution)/shard_map/all_to_all | solution.py:96
  60.3 5.5 %all-to-all-start = ((bf16[64,16,256]{2,1,0:T(8,128)(2,1)}), bf16[64,16,256]{2,1,0:T(8,128)(2,1)S(1)}, u32[]{:S(2)}, u32[]{:S(2)}) async-start(bf16[64,16,256]{2,1,0:T(8,128)(2,1)} %bitcast.11), calls=%async_computation | async-start | bytes 1048576 | tf_op jit(solution)/shard_map/all_to_all | solution.py:94
  65.9 3.8 %convert.6 = bf16[2,2048,256]{2,1,0:T(8,128)(2,1)} convert(f32[2,2048,256]{2,1,0:T(8,128)} %param.28) | non-fusion elementwise | flops 1048576 | bytes 6291456
  70.9 11.7 %all-to-all-done = bf16[64,16,256]{2,1,0:T(8,128)(2,1)S(1)} async-done(((bf16[64,16,256]{2,1,0:T(8,128)(2,1)}), bf16[64,16,256]{2,1,0:T(8,128)(2,1)S(1)}, u32[]{:S(2)}, u32[]{:S(2)}) %all-to-all-start) | async-done | bytes 524320 | tf_op jit(solution)/shard_map/all_to_all | solution.py:94
  82.5 50.4 %while.14 = (s32[]{:T(128)}, f32[2,2048,256]{2,1,0:T(8,128)}, f32[2,2048]{1,0:T(2,128)S(1)}, f32[2,2048]{1,0:T(2,128)S(1)}, bf16[2,2048,256]{2,1,0:T(8,128)(2,1)...) while((s32[]{:T(128)}, f32[2,2048,256]{2,1,0:T(8,128)}, ...), condition=%wide.region_18.19_spmd, body=%wide.region_11.18_spmd.sunk | while | flops 2231370752 | bytes 92651704 | solution.py:130
  82.6 2.5 multiply_reduce_fusion.12
  87.6 2.1 multiply_reduce_fusion.14
  89.7 1.4 fusion.63
  91.2 7.7 %multiply_reduce_fusion.15 = (f32[2048]{0:T(1024)S(1)}, f32[2048]{0:T(1024)S(1)}, f32[2048]{0:T(1024)S(1)}, pred[1024,2048]{1,0:T(32,128)(4,1)}) fusion(f32[1024]{0:T(1024)S(1)} %bitcast.125, f32[1024]{0:T(1024)S(1)} %subtract_multiply_fusion.4, f32[2048]{0:T(1024)S(1)} %bitcast.121, f32[2048]{0:T(1024)S(1)} %add_rsqrt_fusion.2, ...), kind=kLoop, calls=%fused_computation.12.clone.1 | loop fusion | flops 25159680 | bytes 10551296 | tf_op jit(solution)/shard_map/while/body/eval_jaxpr/reduce_sum | solution.py:122
  99.6 8.2 %fusion.62 = f32[2,2048,256]{2,1,0:T(8,128)} fusion(f32[2,2048,256]{2,1,0:T(8,128)} %get-tuple-element.217, s32[]{:T(128)S(6)} %copy.44, bf16[1024,256]{1,0:T(8,128)(2,1)S(1)} %get-tuple-element.235, pred[1024,2048]{1,0:T(32,128)(4,1)} %get-tuple-element.196, f32[2048,1024]{0,1:T(8,128)} %copy-done.1, f32[2048]{0:T(1024)S(1)} %get-tuple-element.199, ...), kind=kOutput, calls=%fused_computation.28.clone.1 | convolution fusion | flops 1094713344 | bytes 13164548 | tf_op jit(solution)/shard_map/while/body/eval_jaxpr/dot_general | solution.py:127
  107.8 2.5 multiply_reduce_fusion.12
  112.9 2.1 multiply_reduce_fusion.14
  114.9 1.4 fusion.63
  116.4 7.7 %multiply_reduce_fusion.15 = (f32[2048]{0:T(1024)S(1)}, f32[2048]{0:T(1024)S(1)}, f32[2048]{0:T(1024)S(1)}, pred[1024,2048]{1,0:T(32,128)(4,1)}) fusion(f32[1024]{0:T(1024)S(1)} %bitcast.125, f32[1024]{0:T(1024)S(1)} %subtract_multiply_fusion.4, f32[2048]{0:T(1024)S(1)} %bitcast.121, f32[2048]{0:T(1024)S(1)} %add_rsqrt_fusion.2, ...), kind=kLoop, calls=%fused_computation.12.clone.1 | loop fusion | flops 25159680 | bytes 10551296 | tf_op jit(solution)/shard_map/while/body/eval_jaxpr/reduce_sum | solution.py:122
  124.8 8.2 %fusion.62 = f32[2,2048,256]{2,1,0:T(8,128)} fusion(f32[2,2048,256]{2,1,0:T(8,128)} %get-tuple-element.217, s32[]{:T(128)S(6)} %copy.44, bf16[1024,256]{1,0:T(8,128)(2,1)S(1)} %get-tuple-element.235, pred[1024,2048]{1,0:T(32,128)(4,1)} %get-tuple-element.196, f32[2048,1024]{0,1:T(8,128)} %copy-done.1, f32[2048]{0:T(1024)S(1)} %get-tuple-element.199, ...), kind=kOutput, calls=%fused_computation.28.clone.1 | convolution fusion | flops 1094713344 | bytes 13164548 | tf_op jit(solution)/shard_map/while/body/eval_jaxpr/dot_general | solution.py:127
  133.0 4.3 %copy.33 = f32[512,2,8,128]{3,1,2,0:T(2,128)S(1)} copy(f32[512,2,8,128]{3,2,1,0:T(8,128)} %bitcast.116) | data formatting | bytes 8388608
  137.3 4.4 %pad_maximum_fusion = f32[1056768]{0:T(1024)} fusion(f32[4096]{0:T(1024)S(1)} %bitcast.129, f32[4096]{0:T(1024)S(1)} %bitcast.130, f32[1048576]{0:T(1024)S(1)} %bitcast.115), kind=kLoop, calls=%fused_computation.43 | loop fusion | flops 2113536 | bytes 8454144 | tf_op jit(solution)/shard_map/concatenate | solution.py:16
  141.7 194.6 %all-reduce.2.cloned.1.call-done = f32[1056768]{0:T(1024)} async-done(((f32[1056768]{0:T(1024)}), f32[1056768]{0:T(1024)}) %all-reduce.2.cloned.1.call-update) | async-done | bytes 4227088 | tf_op jit(solution)/shard_map/psum | solution.py:16
  336.3 3.9 %multiply_reduce_fusion.5 = f32[]{:T(128)} fusion(f32[1056768]{0:T(1024)} %all-reduce.2.cloned.1.call-done), kind=kLoop, calls=%fused_computation.44 | loop fusion | flops 2097151 | bytes 4194308 | tf_op jit(solution)/shard_map/reduce_sum | solution.py:135
  340.2 1.3 multiply_reduce_fusion.6
  343.5 9.3 %all_to_all.36 = f32[4,1,1]{2,1,0:T(1,128)S(1)} all-to-all(f32[4,1,1]{2,1,0:T(1,128)S(1)} %broadcast_in_dim.70), channel_id=1, replica_groups=mesh['dp'=64,'member'=4] {'member'}, dimensions={0} | all-to-all | bytes 32 | tf_op jit(solution)/shard_map/all_to_all | solution.py:22
  354.2 4.4 %slice_multiply_fusion = f32[1048576]{0:T(1024)} fusion(f32[1056768]{0:T(1024)} %all-reduce.2.cloned.1.call-done, f32[]{:T(128)S(6)} %div.42), kind=kLoop, calls=%fused_computation.45 | loop fusion | flops 1048576 | bytes 8388612 | tf_op jit(solution)/shard_map/mul | solution.py:141
  358.6 5.2 %mul.195 = f32[2,2048,256]{2,1,0:T(8,128)} reshape(f32[1048576]{0:T(1024)} %slice_multiply_fusion) | data formatting | bytes 8388608 | tf_op jit(solution)/shard_map/mul | solution.py:141
  (75 shorter events, 14.3 us)
Async XLA Ops:
  7.2 1.6 copy-start
  7.2 11.2 %copy-start.10 = (bf16[8]{0:T(256)(128)(2,1)S(1)}, bf16[8]{0:T(256)(128)(2,1)}, u32[]{:S(2)}) copy-start(bf16[8]{0:T(256)(128)(2,1)} %param.25) | copy-start | bytes 52
  7.2 11.2 %copy-start.5 = (s32[512,2]{0,1:T(2,128)S(1)}, s32[512,2]{0,1:T(2,128)}, u32[]{:S(2)}) copy-start(s32[512,2]{0,1:T(2,128)} %param.26) | copy-start | bytes 12292
  7.2 11.2 %copy-start.4 = (s32[512]{0:T(512)S(1)}, s32[512]{0:T(512)}, u32[]{:S(2)}) copy-start(s32[512]{0:T(512)} %param.27) | copy-start | bytes 6148
  7.2 12.9 %copy-start.6 = (s32[512]{0:T(512)S(1)}, s32[512]{0:T(512)}, u32[]{:S(2)}) copy-start(s32[512]{0:T(512)} %param.24) | copy-start | bytes 6148
  7.2 29.6 %copy-start.7 = (s32[512]{0:T(512)S(1)}, s32[512]{0:T(512)}, u32[]{:S(2)}) copy-start(s32[512]{0:T(512)} %param.23) | copy-start | bytes 6148
  7.2 29.6 %copy-start.8 = (bf16[512]{0:T(512)(128)(2,1)S(1)}, bf16[512]{0:T(512)(128)(2,1)}, u32[]{:S(2)}) copy-start(bf16[512]{0:T(512)(128)(2,1)} %param.22) | copy-start | bytes 3076
  7.2 29.6 %copy-start.9 = (bf16[512]{0:T(512)(128)(2,1)S(1)}, bf16[512]{0:T(512)(128)(2,1)}, u32[]{:S(2)}) copy-start(bf16[512]{0:T(512)(128)(2,1)} %param.21) | copy-start | bytes 3076
  13.5 69.1 %copy-start.2 = (f32[2,2048]{1,0:T(2,128)S(1)}, f32[2,2048]{1,0:T(2,128)}, u32[]{:S(2)}) copy-start(f32[2,2048]{1,0:T(2,128)} %param.29) | copy-start | bytes 49156
  13.5 69.1 %copy-start.3 = (f32[2,2048]{1,0:T(2,128)S(1)}, f32[2,2048]{1,0:T(2,128)}, u32[]{:S(2)}) copy-start(f32[2,2048]{1,0:T(2,128)} %param.30) | copy-start | bytes 49156
  14.1 10.6 %all-to-all-start.2 = ((f32[4,512,2]{1,2,0:T(2,128)}), f32[4,512,2]{1,2,0:T(2,128)S(1)}, u32[]{:S(2)}, u32[]{:S(2)}) async-start(f32[4,512,2]{1,2,0:T(2,128)} %stack.2), calls=%async_computation.2 | async-start | bytes 32768 | tf_op jit(solution)/shard_map/all_to_all | solution.py:83
  24.6 20.7 %all-to-all-start.1 = ((bf16[64,1,16]{2,1,0:T(2,128)(2,1)}), bf16[64,1,16]{2,1,0:T(2,128)(2,1)S(1)}, u32[]{:S(2)}, u32[]{:S(2)}) async-start(bf16[64,1,16]{2,1,0:T(2,128)(2,1)} %all_to_all.29), calls=%async_computation.1 | async-start | bytes 65536 | tf_op jit(solution)/shard_map/all_to_all | solution.py:95
  45.3 15.0 %all-to-all-start.3 = ((bf16[64,1,16]{2,1,0:T(2,128)(2,1)}), bf16[64,1,16]{2,1,0:T(2,128)(2,1)S(1)}, u32[]{:S(2)}, u32[]{:S(2)}) async-start(bf16[64,1,16]{2,1,0:T(2,128)(2,1)} %all_to_all.30), calls=%async_computation.3 | async-start | bytes 65536 | tf_op jit(solution)/shard_map/all_to_all | solution.py:96
  60.3 22.2 %all-to-all-start = ((bf16[64,16,256]{2,1,0:T(8,128)(2,1)}), bf16[64,16,256]{2,1,0:T(8,128)(2,1)S(1)}, u32[]{:S(2)}, u32[]{:S(2)}) async-start(bf16[64,16,256]{2,1,0:T(8,128)(2,1)} %bitcast.11), calls=%async_computation | async-start | bytes 1048576 | tf_op jit(solution)/shard_map/all_to_all | solution.py:94
  65.8 270.5 %all-reduce.2.cloned.1.call-start = ((), (), s32[]{:S(2)}) async-start(), calls=%async_computation.5 | async-start | bytes 8454144 | tf_op jit(solution)/shard_map/psum | solution.py:16
  85.1 4.6 %copy-start.1 = (f32[2048,1024]{0,1:T(8,128)}, f32[2048,1024]{0,1:T(8,128)S(1)}, u32[]{:S(2)}) copy-start(f32[2048,1024]{0,1:T(8,128)S(1)} %get-tuple-element.194) | copy-start | bytes 25165828 | tf_op jit(solution)/shard_map/while
  110.3 4.6 %copy-start.1 = (f32[2048,1024]{0,1:T(8,128)}, f32[2048,1024]{0,1:T(8,128)S(1)}, u32[]{:S(2)}) copy-start(f32[2048,1024]{0,1:T(8,128)S(1)} %get-tuple-element.194) | copy-start | bytes 25165828 | tf_op jit(solution)/shard_map/while
Sparse Core Ops, SparseCore 0:
  141.8 194.4 all-reduce.1
